TPU v7x, 256 devices: a whole 4x4x8 slice. The times are simulated.
256 devices in a mesh: dp: 32 (over x, y, core), tensor: 8 (over z).
Axes of the slice: x: 4, y: 4, z: 8, core: 2. Of those that a mesh axis runs over, the one named last changes fastest.
Arguments:
- img_hidden: bfloat16 [32768, 4304], P('dp', 'tensor'), may hold values from -0.25 to 0.25
- img_down: bfloat16 [4304, 1152], P('tensor'), may hold values from -0.09375 to 0.09375
- img_pooled: bfloat16 [32768, 1152], P(('dp', 'tensor')), may hold values from -0.25 to 0.25
- txt_hidden: bfloat16 [32768, 1152], P('dp', 'tensor'), may hold values from -0.25 to 0.25
- txt_proj: bfloat16 [1152, 1152], P('tensor'), may hold values from -0.1875 to 0.1875
- log_temp: float32 [1], replicated, may hold values from 1 to 2
- bias: float32 [1], replicated, may hold values from -4 to -1
- match: int32 [32768], P(('dp', 'tensor')), may hold values from 0 to 32767
- window_index: int32 [1], replicated, may hold values from 0 to 15
Outputs:
- img_grad: float32 [32768, 1152], P(('dp', 'tensor'))
- txt_grad: float32 [32768, 1152], P(('dp', 'tensor'))
- row_loss: float32 [32768], P(('dp', 'tensor'))
All inputs are finite; a program needn't handle non-finite values.
Results may differ from a plain program's by a relative error of at most 0.0039.
Values may be sent and summed in bfloat16 or wider, within the bound.
No kernel may reach another device: no remote copies, remote signals or barrier semaphores. Data moves between devices by JAX's collectives and lax.ppermute only.
A program may use at most 64 MiB of HBM per device.

v0:
```python
import jax
import jax.numpy as jnp
from jax import lax
from jax.sharding import PartitionSpec as P

STEPS = 16


def shifted(shard, axis, by):
    devices = lax.axis_size(axis)
    return lax.ppermute(shard, axis, [(i, (i + by) % devices) for i in range(devices)])


def unit_rows(emb):
    length = jnp.sqrt(jnp.sum(emb * emb, axis=1, keepdims=True) + 1e-06)
    return (emb / length, length)


def pair_tile(image_low, text_block, owner, match, scale, shift_value):
    cosine = lax.dot_general(
        image_low, text_block, (((1,), (1,)), ((), ())), preferred_element_type=jnp.float32
    )
    text_index = owner * text_block.shape[0] + lax.iota(jnp.int32, text_block.shape[0])
    positive = match[:, None] == text_index[None, :]
    logit = scale * cosine + shift_value
    pair_loss = jnp.sum(
        jnp.where(positive, jax.nn.softplus(-logit), jax.nn.softplus(logit)), axis=1
    )
    coef = ((jax.nn.sigmoid(logit) - positive.astype(jnp.float32)) * scale).astype(jnp.bfloat16)
    image_part = jnp.dot(coef, text_block, preferred_element_type=jnp.float32)
    text_part = lax.dot_general(
        coef, image_low, (((0,), (0,)), ((), ())), preferred_element_type=jnp.float32
    )
    return (pair_loss, image_part, text_part)


def offset_blocks(blocks, window):
    windows = lax.axis_size(("dp", "tensor")) // STEPS
    for level in range((windows - 1).bit_length()):
        moved = shifted(blocks, ("dp", "tensor"), STEPS << level)
        blocks = jnp.where(window >> level & 1 == 1, moved, blocks)
    return blocks


def return_home(text_sum, fixed_steps, window):
    text_sum = shifted(text_sum, ("dp", "tensor"), -fixed_steps)
    windows = lax.axis_size(("dp", "tensor")) // STEPS
    for level in range((windows - 1).bit_length()):
        moved = shifted(text_sum, ("dp", "tensor"), -(STEPS << level))
        text_sum = jnp.where(window >> level & 1 == 1, moved, text_sum)
    return text_sum


def body(
    img_hidden, img_down, img_pooled, txt_hidden, txt_proj, log_temp, bias, match, window_index
):
    width = img_pooled.shape[1]
    summed = lax.psum_scatter(
        jnp.concatenate(
            [
                jnp.dot(img_hidden, img_down, preferred_element_type=jnp.float32),
                jnp.dot(txt_hidden, txt_proj, preferred_element_type=jnp.float32),
            ],
            axis=1,
        ),
        "tensor",
        scatter_dimension=0,
        tiled=True,
    )
    img_emb = summed[:, :width] + img_pooled.astype(jnp.float32)
    txt_emb = summed[:, width:]
    img_unit, img_len = unit_rows(img_emb)
    txt_unit, txt_len = unit_rows(txt_emb)
    image_low = img_unit.astype(jnp.bfloat16)
    text_low = txt_unit.astype(jnp.bfloat16)
    scale = jnp.exp(log_temp[0])
    shift_value = bias[0]
    window = window_index[0]
    start_step = window * STEPS
    position = lax.axis_index(("dp", "tensor"))
    devices = lax.axis_size(("dp", "tensor"))
    half_steps = STEPS // 2
    late_copy = shifted(text_low, ("dp", "tensor"), STEPS - 1)
    stacked = offset_blocks(jnp.stack([text_low, late_copy]), window)
    early_block = stacked[0]
    late_block = stacked[1]
    early_owner = (position - start_step) % devices
    late_owner = (position - start_step - (STEPS - 1)) % devices
    early_loss, early_image, early_sum = pair_tile(
        image_low, early_block, early_owner, match, scale, shift_value
    )
    late_loss, late_image, late_sum = pair_tile(
        image_low, late_block, late_owner, match, scale, shift_value
    )

    def two_turn(turn, carry):
        early_now, late_now, early_acc, late_acc, image_now, loss_now = carry
        early_now = shifted(early_now, ("dp", "tensor"), 1)
        late_now = shifted(late_now, ("dp", "tensor"), -1)
        early_acc = shifted(early_acc, ("dp", "tensor"), 1)
        late_acc = shifted(late_acc, ("dp", "tensor"), -1)
        owner_early = (position - start_step - turn) % devices
        owner_late = (position - start_step - (STEPS - 1) + turn) % devices
        loss_one, image_one, text_one = pair_tile(
            image_low, early_now, owner_early, match, scale, shift_value
        )
        loss_two, image_two, text_two = pair_tile(
            image_low, late_now, owner_late, match, scale, shift_value
        )
        return (
            early_now,
            late_now,
            early_acc + text_one,
            late_acc + text_two,
            image_now + image_one + image_two,
            loss_now + loss_one + loss_two,
        )

    carried = lax.fori_loop(
        1,
        half_steps,
        two_turn,
        (
            early_block,
            late_block,
            early_sum,
            late_sum,
            early_image + late_image,
            early_loss + late_loss,
        ),
    )
    early_sum = carried[2]
    late_sum = carried[3]
    image_dunit = carried[4]
    row_loss = carried[5]
    late_moved = shifted(late_sum, ("dp", "tensor"), -1)
    text_dunit = return_home(early_sum + late_moved, half_steps - 1, window)
    img_grad = (
        image_dunit - img_unit * jnp.sum(img_unit * image_dunit, axis=1, keepdims=True)
    ) / img_len
    txt_grad = (
        text_dunit - txt_unit * jnp.sum(txt_unit * text_dunit, axis=1, keepdims=True)
    ) / txt_len
    return (img_grad, txt_grad, row_loss)


def solution(mesh):
    in_specs = (
        P("dp", "tensor"),
        P("tensor", None),
        P(("dp", "tensor"), None),
        P("dp", "tensor"),
        P("tensor", None),
        P(),
        P(),
        P(("dp", "tensor")),
        P(),
    )
    out_specs = (P(("dp", "tensor"), None), P(("dp", "tensor"), None), P(("dp", "tensor")))
    return jax.shard_map(body, mesh=mesh, in_specs=in_specs, out_specs=out_specs, check_vma=False)
```

profile of v0, /device:TPU:192, one launch (start us, length us, event | category | flops | bytes accessed | tf_op | source)
XLA Modules:
  0.0 485.2 jit_solution(13462369484042464486)
XLA Ops:
  8.5 5.7 %fusion.44 = f32[1024,1152]{1,0:T(8,128)} fusion(bf16[1024,538]{0,1:T(8,128)(2,1)} %param.11, bf16[538,1152]{1,0:T(8,128)(2,1)S(1)} %copy-done), kind=kOutput, calls=%fused_computation.95 | convolution fusion | flops 1269301248 | bytes 7059968 | tf_op jit(solution)/shard_map/dot_general | solution.py:61
  15.0 6.7 %pad_maximum_fusion = f32[1024,2304]{1,0:T(8,128)} fusion(f32[1024,1152]{1,0:T(8,128)S(1)} %fusion.45, f32[1024,1152]{1,0:T(8,128)} %fusion.44), kind=kLoop, calls=%fused_computation.36 | loop fusion | flops 2359296 | bytes 18874368 | tf_op jit(solution)/shard_map/concatenate | solution.py:59
  21.8 103.8 %reduce-scatter.2.cloned.1.call-done = f32[128,2304]{1,0:T(8,128)} async-done(((f32[1024,2304]{1,0:T(8,128)}), f32[128,2304]{1,0:T(8,128)}) %reduce-scatter.2.cloned.1.call-update) | async-done | bytes 1179664 | tf_op jit(solution)/shard_map/reduce_scatter | solution.py:58
  127.4 2.4 collective-permute-start.4
  129.8 10.6 %collective-permute-done.4 = bf16[128,1152]{1,0:T(8,128)(2,1)S(1)} collective-permute-done((bf16[128,1152]{1,0:T(8,128)(2,1)S(1)}, bf16[128,1152]{1,0:T(8,128)(2,1)S(1)}, u32[]{:S(2)}, u32[]{:S(2)}) %collective-permute-start.4) | collective-permute-done | bytes 294944 | tf_op jit(solution)/shard_map/ppermute | solution.py:11
  141.2 16.8 %collective-permute-done.5 = bf16[2,128,1152]{2,1,0:T(8,128)(2,1)S(1)} collective-permute-done((bf16[2,128,1152]{2,1,0:T(8,128)(2,1)S(1)}, bf16[2,128,1152]{2,1,0:T(8,128)(2,1)S(1)}, u32[]{:S(2)}, u32[]{:S(2)}) %collective-permute-start.5) | collective-permute-done | bytes 589856 | tf_op jit(solution)/shard_map/ppermute | solution.py:11
  158.1 17.8 %collective-permute-done.6 = bf16[2,128,1152]{2,1,0:T(8,128)(2,1)S(1)} collective-permute-done((bf16[2,128,1152]{2,1,0:T(8,128)(2,1)S(1)}, bf16[2,128,1152]{2,1,0:T(8,128)(2,1)S(1)}, u32[]{:S(2)}, u32[]{:S(2)}) %collective-permute-start.6) | collective-permute-done | bytes 589856 | tf_op jit(solution)/shard_map/ppermute | solution.py:11
  176.1 19.0 %collective-permute-done.7 = bf16[2,128,1152]{2,1,0:T(8,128)(2,1)S(1)} collective-permute-done((bf16[2,128,1152]{2,1,0:T(8,128)(2,1)S(1)}, bf16[2,128,1152]{2,1,0:T(8,128)(2,1)S(1)}, u32[]{:S(2)}, u32[]{:S(2)}) %collective-permute-start.7) | collective-permute-done | bytes 589856 | tf_op jit(solution)/shard_map/ppermute | solution.py:11
  196.9 10.0 %collective-permute-done.8 = bf16[2,128,1152]{2,1,0:T(8,128)(2,1)S(1)} collective-permute-done((bf16[2,128,1152]{2,1,0:T(8,128)(2,1)S(1)}, bf16[2,128,1152]{2,1,0:T(8,128)(2,1)S(1)}, u32[]{:S(2)}, u32[]{:S(2)}) %collective-permute-start.8) | collective-permute-done | bytes 589856 | tf_op jit(solution)/shard_map/ppermute | solution.py:11
  211.3 169.5 %while.25 = (s32[]{:T(128)}, bf16[128,1152]{1,0:T(8,128)(2,1)}, bf16[128,1152]{1,0:T(8,128)(2,1)}, f32[128,1152]{1,0:T(8,128)}, f32[128,1152]{1,0:T(8,128)}, /*i...) while((s32[]{:T(128)}, bf16[128,1152]{1,0:T(8,128)(2,1)}, ...), condition=%wide.region_8.9_spmd, body=%wide.region_5.8_spmd.sunk | while | flops 228196640 | bytes 15804535 | solution.py:119
  215.4 3.2 collective-permute-done.1
  222.7 6.7 %collective-permute-done.2 = f32[128,1152]{1,0:T(8,128)} collective-permute-done((f32[128,1152]{1,0:T(8,128)}, f32[128,1152]{1,0:T(8,128)}, u32[]{:S(2)}, u32[]{:S(2)}) %collective-permute-start.2) | collective-permute-done | bytes 589856 | tf_op jit(solution)/shard_map/while/body/eval_jaxpr/ppermute | solution.py:11
  229.3 2.2 convolution_add_fusion.6
  232.6 3.5 collective-permute-start.1
  236.1 4.4 collective-permute-start.3
  240.5 2.2 collective-permute-done.1
  248.2 5.0 %collective-permute-done.2 = f32[128,1152]{1,0:T(8,128)} collective-permute-done((f32[128,1152]{1,0:T(8,128)}, f32[128,1152]{1,0:T(8,128)}, u32[]{:S(2)}, u32[]{:S(2)}) %collective-permute-start.2) | collective-permute-done | bytes 589856 | tf_op jit(solution)/shard_map/while/body/eval_jaxpr/ppermute | solution.py:11
  253.2 2.2 convolution_add_fusion.6
  256.5 7.5 %collective-permute-start.1 = (bf16[128,1152]{1,0:T(8,128)(2,1)}, bf16[128,1152]{1,0:T(8,128)(2,1)S(1)}, u32[]{:S(2)}, u32[]{:S(2)}) collective-permute-start(bf16[128,1152]{1,0:T(8,128)(2,1)} %get-tuple-element.481), channel_id=1, source_target_pairs={{0,255},{1,0},{2,1},{3,2},{4,3},{5,4},{6,5},{7,6},{8,7},{9,8},{10,... | collective-permute-start | bytes 884744 | tf_op jit(solution)/shard_map/while/body/eval_jaxpr/ppermute | solution.py:11
  263.9 2.0 collective-permute-start.3
  266.0 2.5 collective-permute-done.1
  273.7 4.9 %collective-permute-done.2 = f32[128,1152]{1,0:T(8,128)} collective-permute-done((f32[128,1152]{1,0:T(8,128)}, f32[128,1152]{1,0:T(8,128)}, u32[]{:S(2)}, u32[]{:S(2)}) %collective-permute-start.2) | collective-permute-done | bytes 589856 | tf_op jit(solution)/shard_map/while/body/eval_jaxpr/ppermute | solution.py:11
  278.6 2.2 convolution_add_fusion.6
  281.8 3.0 collective-permute-start.1
  286.9 4.6 collective-permute-done.1
  295.6 2.6 collective-permute-done.2
  298.2 2.2 convolution_add_fusion.6
  304.5 3.4 collective-permute-start.2
  308.0 3.4 collective-permute-done.1
  315.6 7.8 %collective-permute-done.2 = f32[128,1152]{1,0:T(8,128)} collective-permute-done((f32[128,1152]{1,0:T(8,128)}, f32[128,1152]{1,0:T(8,128)}, u32[]{:S(2)}, u32[]{:S(2)}) %collective-permute-start.2) | collective-permute-done | bytes 589856 | tf_op jit(solution)/shard_map/while/body/eval_jaxpr/ppermute | solution.py:11
  323.4 2.2 convolution_add_fusion.6
  326.7 4.3 collective-permute-start
  331.0 3.4 collective-permute-start.2
  334.4 3.5 collective-permute-done.1
  342.0 7.9 %collective-permute-done.2 = f32[128,1152]{1,0:T(8,128)} collective-permute-done((f32[128,1152]{1,0:T(8,128)}, f32[128,1152]{1,0:T(8,128)}, u32[]{:S(2)}, u32[]{:S(2)}) %collective-permute-start.2) | collective-permute-done | bytes 589856 | tf_op jit(solution)/shard_map/while/body/eval_jaxpr/ppermute | solution.py:11
  349.9 2.2 convolution_add_fusion.6
  353.2 4.8 collective-permute-start
  358.0 3.4 collective-permute-start.2
  361.4 4.1 collective-permute-done.1
  369.6 7.9 %collective-permute-done.2 = f32[128,1152]{1,0:T(8,128)} collective-permute-done((f32[128,1152]{1,0:T(8,128)}, f32[128,1152]{1,0:T(8,128)}, u32[]{:S(2)}, u32[]{:S(2)}) %collective-permute-start.2) | collective-permute-done | bytes 589856 | tf_op jit(solution)/shard_map/while/body/eval_jaxpr/ppermute | solution.py:11
  377.6 2.2 convolution_add_fusion.6
  380.8 17.9 %collective-permute-done.9 = f32[128,1152]{1,0:T(8,128)S(1)} collective-permute-done((f32[128,1152]{1,0:T(8,128)}, f32[128,1152]{1,0:T(8,128)S(1)}, u32[]{:S(2)}, u32[]{:S(2)}) %collective-permute-start.9) | collective-permute-done | bytes 589856 | tf_op jit(solution)/shard_map/ppermute | solution.py:11
  399.9 6.6 %collective-permute-start.10 = (f32[128,1152]{1,0:T(8,128)S(1)}, f32[128,1152]{1,0:T(8,128)S(1)}, u32[]{:S(2)}, u32[]{:S(2)}) collective-permute-start(f32[128,1152]{1,0:T(8,128)S(1)} %add.355), channel_id=1, source_target_pairs={{0,249},{1,250},{2,251},{3,252},{4,253},{5,254},{6,255},{7,0},{8,1... | collective-permute-start | bytes 1769480 | tf_op jit(solution)/shard_map/ppermute | solution.py:11
  406.6 8.6 %collective-permute-done.10 = f32[128,1152]{1,0:T(8,128)S(1)} collective-permute-done((f32[128,1152]{1,0:T(8,128)S(1)}, f32[128,1152]{1,0:T(8,128)S(1)}, u32[]{:S(2)}, u32[]{:S(2)}) %collective-permute-start.10) | collective-permute-done | bytes 589856 | tf_op jit(solution)/shard_map/ppermute | solution.py:11
  415.2 16.2 %collective-permute-done.11 = f32[128,1152]{1,0:T(8,128)S(1)} collective-permute-done((f32[128,1152]{1,0:T(8,128)S(1)}, f32[128,1152]{1,0:T(8,128)S(1)}, u32[]{:S(2)}, u32[]{:S(2)}) %collective-permute-start.11) | collective-permute-done | bytes 589856 | tf_op jit(solution)/shard_map/ppermute | solution.py:11
  431.5 16.3 %collective-permute-done.12 = f32[128,1152]{1,0:T(8,128)S(1)} collective-permute-done((f32[128,1152]{1,0:T(8,128)S(1)}, f32[128,1152]{1,0:T(8,128)S(1)}, u32[]{:S(2)}, u32[]{:S(2)}) %collective-permute-start.12) | collective-permute-done | bytes 589856 | tf_op jit(solution)/shard_map/ppermute | solution.py:11
  448.4 13.5 %collective-permute-done.13 = f32[128,1152]{1,0:T(8,128)S(1)} collective-permute-done((f32[128,1152]{1,0:T(8,128)S(1)}, f32[128,1152]{1,0:T(8,128)S(1)}, u32[]{:S(2)}, u32[]{:S(2)}) %collective-permute-start.13) | collective-permute-done | bytes 589856 | tf_op jit(solution)/shard_map/ppermute | solution.py:11
  463.3 13.3 %collective-permute-done.14 = f32[128,1152]{1,0:T(8,128)S(1)} collective-permute-done((f32[128,1152]{1,0:T(8,128)S(1)}, f32[128,1152]{1,0:T(8,128)S(1)}, u32[]{:S(2)}, u32[]{:S(2)}) %collective-permute-start.14) | collective-permute-done | bytes 589856 | tf_op jit(solution)/shard_map/ppermute | solution.py:11
  (148 shorter events, 62.4 us)
Async XLA Ops:
  7.2 6.9 %copy-start.7 = (bf16[1024,144]{0,1:T(8,128)(2,1)S(1)}, bf16[1024,144]{0,1:T(8,128)(2,1)}, u32[]{:S(2)}) copy-start(bf16[1024,144]{0,1:T(8,128)(2,1)} %param.14) | copy-start | bytes 884740
  7.2 6.9 %copy-start.5 = (bf16[144,1152]{1,0:T(8,128)(2,1)S(1)}, bf16[144,1152]{1,0:T(8,128)(2,1)}, u32[]{:S(2)}) copy-start(bf16[144,1152]{1,0:T(8,128)(2,1)} %param.15) | copy-start | bytes 995332
  7.2 118.4 %reduce-scatter.2.cloned.1.call-start = ((), (), s32[]{:S(2)}) async-start(), calls=%async_computation.1 | async-start | bytes 10616832 | tf_op jit(solution)/shard_map/reduce_scatter | solution.py:58
  21.7 103.9 %copy-start.3 = (bf16[128,1152]{1,0:T(8,128)(2,1)S(1)}, bf16[128,1152]{1,0:T(8,128)(2,1)}, u32[]{:S(2)}) copy-start(bf16[128,1152]{1,0:T(8,128)(2,1)} %param.13) | copy-start | bytes 884740
  125.6 1.6 copy-start.1
  127.4 13.0 %collective-permute-start.4 = (bf16[128,1152]{1,0:T(8,128)(2,1)S(1)}, bf16[128,1152]{1,0:T(8,128)(2,1)S(1)}, u32[]{:S(2)}, u32[]{:S(2)}) collective-permute-start(bf16[128,1152]{1,0:T(8,128)(2,1)S(1)} %get-tuple-element.364), channel_id=1, source_target_pairs={{0,15},{1,16},{2,17},{3,18},{4,19},{5,20},{6,21},{7,22},{8,23},{9,... | collective-permute-start | bytes 884744 | tf_op jit(solution)/shard_map/ppermute | solution.py:11
  140.4 17.5 %collective-permute-start.5 = (bf16[2,128,1152]{2,1,0:T(8,128)(2,1)S(1)}, bf16[2,128,1152]{2,1,0:T(8,128)(2,1)S(1)}, u32[]{:S(2)}, u32[]{:S(2)}) collective-permute-start(bf16[2,128,1152]{2,1,0:T(8,128)(2,1)S(1)} %pad_maximum_fusion.1), channel_id=1, source_target_pairs={{0,16},{1,17},{2,18},{3,19},{4,20},{5,21},{6,22},{7,23},{8,24},{9,... | collective-permute-start | bytes 1769480 | tf_op jit(solution)/shard_map/ppermute | solution.py:11
  158.0 17.9 %collective-permute-start.6 = (bf16[2,128,1152]{2,1,0:T(8,128)(2,1)S(1)}, bf16[2,128,1152]{2,1,0:T(8,128)(2,1)S(1)}, u32[]{:S(2)}, u32[]{:S(2)}) collective-permute-start(bf16[2,128,1152]{2,1,0:T(8,128)(2,1)S(1)} %broadcast_select_fusion), channel_id=1, source_target_pairs={{0,32},{1,33},{2,34},{3,35},{4,36},{5,37},{6,38},{7,39},{8,40},{9,... | collective-permute-start | bytes 1769480 | tf_op jit(solution)/shard_map/ppermute | solution.py:11
  176.0 19.1 %collective-permute-start.7 = (bf16[2,128,1152]{2,1,0:T(8,128)(2,1)S(1)}, bf16[2,128,1152]{2,1,0:T(8,128)(2,1)S(1)}, u32[]{:S(2)}, u32[]{:S(2)}) collective-permute-start(bf16[2,128,1152]{2,1,0:T(8,128)(2,1)S(1)} %broadcast_select_fusion.1), channel_id=1, source_target_pairs={{0,64},{1,65},{2,66},{3,67},{4,68},{5,69},{6,70},{7,71},{8,72},{9,... | collective-permute-start | bytes 1769480 | tf_op jit(solution)/shard_map/ppermute | solution.py:11
  195.2 11.7 %collective-permute-start.8 = (bf16[2,128,1152]{2,1,0:T(8,128)(2,1)S(1)}, bf16[2,128,1152]{2,1,0:T(8,128)(2,1)S(1)}, u32[]{:S(2)}, u32[]{:S(2)}) collective-permute-start(bf16[2,128,1152]{2,1,0:T(8,128)(2,1)S(1)} %broadcast_select_fusion.2), channel_id=1, source_target_pairs={{0,128},{1,129},{2,130},{3,131},{4,132},{5,133},{6,134},{7,135},{8... | collective-permute-start | bytes 1769480 | tf_op jit(solution)/shard_map/ppermute | solution.py:11
  195.5 11.7 %copy-start.6 = (s32[128]{0:T(128)S(1)}, s32[128]{0:T(128)}, u32[]{:S(2)}) copy-start(s32[128]{0:T(128)} %param.18) | copy-start | bytes 1540
  211.3 7.3 %collective-permute-start.1 = (bf16[128,1152]{1,0:T(8,128)(2,1)}, bf16[128,1152]{1,0:T(8,128)(2,1)S(1)}, u32[]{:S(2)}, u32[]{:S(2)}) collective-permute-start(bf16[128,1152]{1,0:T(8,128)(2,1)} %get-tuple-element.481), channel_id=1, source_target_pairs={{0,255},{1,0},{2,1},{3,2},{4,3},{5,4},{6,5},{7,6},{8,7},{9,8},{10,... | collective-permute-start | bytes 884744 | tf_op jit(solution)/shard_map/while/body/eval_jaxpr/ppermute | solution.py:11
  212.8 7.0 %collective-permute-start = (bf16[128,1152]{1,0:T(8,128)(2,1)}, bf16[128,1152]{1,0:T(8,128)(2,1)S(1)}, u32[]{:S(2)}, u32[]{:S(2)}) collective-permute-start(bf16[128,1152]{1,0:T(8,128)(2,1)} %get-tuple-element.480), channel_id=1, source_target_pairs={{0,1},{1,2},{2,3},{3,4},{4,5},{5,6},{6,7},{7,8},{8,9},{9,10},{10,1... | collective-permute-start | bytes 884744 | tf_op jit(solution)/shard_map/while/body/eval_jaxpr/ppermute | solution.py:11
  213.4 15.9 %collective-permute-start.2 = (f32[128,1152]{1,0:T(8,128)}, f32[128,1152]{1,0:T(8,128)}, u32[]{:S(2)}, u32[]{:S(2)}) collective-permute-start(f32[128,1152]{1,0:T(8,128)} %get-tuple-element.482), channel_id=1, source_target_pairs={{0,1},{1,2},{2,3},{3,4},{4,5},{5,6},{6,7},{7,8},{8,9},{9,10},{10,1... | collective-permute-start | bytes 1769480 | tf_op jit(solution)/shard_map/while/body/eval_jaxpr/ppermute | solution.py:11
  213.4 18.1 %collective-permute-start.3 = (f32[128,1152]{1,0:T(8,128)}, f32[128,1152]{1,0:T(8,128)S(1)}, u32[]{:S(2)}, u32[]{:S(2)}) collective-permute-start(f32[128,1152]{1,0:T(8,128)} %get-tuple-element.483), channel_id=1, source_target_pairs={{0,255},{1,0},{2,1},{3,2},{4,3},{5,4},{6,5},{7,6},{8,7},{9,8},{10,... | collective-permute-start | bytes 1769480 | tf_op jit(solution)/shard_map/while/body/eval_jaxpr/ppermute | solution.py:11
  232.6 10.1 %collective-permute-start.1 = (bf16[128,1152]{1,0:T(8,128)(2,1)}, bf16[128,1152]{1,0:T(8,128)(2,1)S(1)}, u32[]{:S(2)}, u32[]{:S(2)}) collective-permute-start(bf16[128,1152]{1,0:T(8,128)(2,1)} %get-tuple-element.481), channel_id=1, source_target_pairs={{0,255},{1,0},{2,1},{3,2},{4,3},{5,4},{6,5},{7,6},{8,7},{9,8},{10,... | collective-permute-start | bytes 884744 | tf_op jit(solution)/shard_map/while/body/eval_jaxpr/ppermute | solution.py:11
  236.1 9.3 %collective-permute-start = (bf16[128,1152]{1,0:T(8,128)(2,1)}, bf16[128,1152]{1,0:T(8,128)(2,1)S(1)}, u32[]{:S(2)}, u32[]{:S(2)}) collective-permute-start(bf16[128,1152]{1,0:T(8,128)(2,1)} %get-tuple-element.480), channel_id=1, source_target_pairs={{0,1},{1,2},{2,3},{3,4},{4,5},{5,6},{6,7},{7,8},{8,9},{9,10},{10,1... | collective-permute-start | bytes 884744 | tf_op jit(solution)/shard_map/while/body/eval_jaxpr/ppermute | solution.py:11
  236.1 17.1 %collective-permute-start.2 = (f32[128,1152]{1,0:T(8,128)}, f32[128,1152]{1,0:T(8,128)}, u32[]{:S(2)}, u32[]{:S(2)}) collective-permute-start(f32[128,1152]{1,0:T(8,128)} %get-tuple-element.482), channel_id=1, source_target_pairs={{0,1},{1,2},{2,3},{3,4},{4,5},{5,6},{6,7},{7,8},{8,9},{9,10},{10,1... | collective-permute-start | bytes 1769480 | tf_op jit(solution)/shard_map/while/body/eval_jaxpr/ppermute | solution.py:11
  236.1 19.2 %collective-permute-start.3 = (f32[128,1152]{1,0:T(8,128)}, f32[128,1152]{1,0:T(8,128)S(1)}, u32[]{:S(2)}, u32[]{:S(2)}) collective-permute-start(f32[128,1152]{1,0:T(8,128)} %get-tuple-element.483), channel_id=1, source_target_pairs={{0,255},{1,0},{2,1},{3,2},{4,3},{5,4},{6,5},{7,6},{8,7},{9,8},{10,... | collective-permute-start | bytes 1769480 | tf_op jit(solution)/shard_map/while/body/eval_jaxpr/ppermute | solution.py:11
  256.5 12.0 %collective-permute-start.1 = (bf16[128,1152]{1,0:T(8,128)(2,1)}, bf16[128,1152]{1,0:T(8,128)(2,1)S(1)}, u32[]{:S(2)}, u32[]{:S(2)}) collective-permute-start(bf16[128,1152]{1,0:T(8,128)(2,1)} %get-tuple-element.481), channel_id=1, source_target_pairs={{0,255},{1,0},{2,1},{3,2},{4,3},{5,4},{6,5},{7,6},{8,7},{9,8},{10,... | collective-permute-start | bytes 884744 | tf_op jit(solution)/shard_map/while/body/eval_jaxpr/ppermute | solution.py:11
  263.9 6.9 %collective-permute-start = (bf16[128,1152]{1,0:T(8,128)(2,1)}, bf16[128,1152]{1,0:T(8,128)(2,1)S(1)}, u32[]{:S(2)}, u32[]{:S(2)}) collective-permute-start(bf16[128,1152]{1,0:T(8,128)(2,1)} %get-tuple-element.480), channel_id=1, source_target_pairs={{0,1},{1,2},{2,3},{3,4},{4,5},{5,6},{6,7},{7,8},{8,9},{9,10},{10,1... | collective-permute-start | bytes 884744 | tf_op jit(solution)/shard_map/while/body/eval_jaxpr/ppermute | solution.py:11
  263.9 14.7 %collective-permute-start.2 = (f32[128,1152]{1,0:T(8,128)}, f32[128,1152]{1,0:T(8,128)}, u32[]{:S(2)}, u32[]{:S(2)}) collective-permute-start(f32[128,1152]{1,0:T(8,128)} %get-tuple-element.482), channel_id=1, source_target_pairs={{0,1},{1,2},{2,3},{3,4},{4,5},{5,6},{6,7},{7,8},{8,9},{9,10},{10,1... | collective-permute-start | bytes 1769480 | tf_op jit(solution)/shard_map/while/body/eval_jaxpr/ppermute | solution.py:11
  263.9 16.8 %collective-permute-start.3 = (f32[128,1152]{1,0:T(8,128)}, f32[128,1152]{1,0:T(8,128)S(1)}, u32[]{:S(2)}, u32[]{:S(2)}) collective-permute-start(f32[128,1152]{1,0:T(8,128)} %get-tuple-element.483), channel_id=1, source_target_pairs={{0,255},{1,0},{2,1},{3,2},{4,3},{5,4},{6,5},{7,6},{8,7},{9,8},{10,... | collective-permute-start | bytes 1769480 | tf_op jit(solution)/shard_map/while/body/eval_jaxpr/ppermute | solution.py:11
  281.8 9.7 %collective-permute-start.1 = (bf16[128,1152]{1,0:T(8,128)(2,1)}, bf16[128,1152]{1,0:T(8,128)(2,1)S(1)}, u32[]{:S(2)}, u32[]{:S(2)}) collective-permute-start(bf16[128,1152]{1,0:T(8,128)(2,1)} %get-tuple-element.481), channel_id=1, source_target_pairs={{0,255},{1,0},{2,1},{3,2},{4,3},{5,4},{6,5},{7,6},{8,7},{9,8},{10,... | collective-permute-start | bytes 884744 | tf_op jit(solution)/shard_map/while/body/eval_jaxpr/ppermute | solution.py:11
  284.8 7.9 %collective-permute-start = (bf16[128,1152]{1,0:T(8,128)(2,1)}, bf16[128,1152]{1,0:T(8,128)(2,1)S(1)}, u32[]{:S(2)}, u32[]{:S(2)}) collective-permute-start(bf16[128,1152]{1,0:T(8,128)(2,1)} %get-tuple-element.480), channel_id=1, source_target_pairs={{0,1},{1,2},{2,3},{3,4},{4,5},{5,6},{6,7},{7,8},{8,9},{9,10},{10,1... | collective-permute-start | bytes 884744 | tf_op jit(solution)/shard_map/while/body/eval_jaxpr/ppermute | solution.py:11
  284.8 13.4 %collective-permute-start.2 = (f32[128,1152]{1,0:T(8,128)}, f32[128,1152]{1,0:T(8,128)}, u32[]{:S(2)}, u32[]{:S(2)}) collective-permute-start(f32[128,1152]{1,0:T(8,128)} %get-tuple-element.482), channel_id=1, source_target_pairs={{0,1},{1,2},{2,3},{3,4},{4,5},{5,6},{6,7},{7,8},{8,9},{9,10},{10,1... | collective-permute-start | bytes 1769480 | tf_op jit(solution)/shard_map/while/body/eval_jaxpr/ppermute | solution.py:11
  284.8 16.6 %collective-permute-start.3 = (f32[128,1152]{1,0:T(8,128)}, f32[128,1152]{1,0:T(8,128)S(1)}, u32[]{:S(2)}, u32[]{:S(2)}) collective-permute-start(f32[128,1152]{1,0:T(8,128)} %get-tuple-element.483), channel_id=1, source_target_pairs={{0,255},{1,0},{2,1},{3,2},{4,3},{5,4},{6,5},{7,6},{8,7},{9,8},{10,... | collective-permute-start | bytes 1769480 | tf_op jit(solution)/shard_map/while/body/eval_jaxpr/ppermute | solution.py:11
  302.5 8.9 %collective-permute-start.1 = (bf16[128,1152]{1,0:T(8,128)(2,1)}, bf16[128,1152]{1,0:T(8,128)(2,1)S(1)}, u32[]{:S(2)}, u32[]{:S(2)}) collective-permute-start(bf16[128,1152]{1,0:T(8,128)(2,1)} %get-tuple-element.481), channel_id=1, source_target_pairs={{0,255},{1,0},{2,1},{3,2},{4,3},{5,4},{6,5},{7,6},{8,7},{9,8},{10,... | collective-permute-start | bytes 884744 | tf_op jit(solution)/shard_map/while/body/eval_jaxpr/ppermute | solution.py:11
  302.5 10.3 %collective-permute-start = (bf16[128,1152]{1,0:T(8,128)(2,1)}, bf16[128,1152]{1,0:T(8,128)(2,1)S(1)}, u32[]{:S(2)}, u32[]{:S(2)}) collective-permute-start(bf16[128,1152]{1,0:T(8,128)(2,1)} %get-tuple-element.480), channel_id=1, source_target_pairs={{0,1},{1,2},{2,3},{3,4},{4,5},{5,6},{6,7},{7,8},{8,9},{9,10},{10,1... | collective-permute-start | bytes 884744 | tf_op jit(solution)/shard_map/while/body/eval_jaxpr/ppermute | solution.py:11
  304.5 18.9 %collective-permute-start.2 = (f32[128,1152]{1,0:T(8,128)}, f32[128,1152]{1,0:T(8,128)}, u32[]{:S(2)}, u32[]{:S(2)}) collective-permute-start(f32[128,1152]{1,0:T(8,128)} %get-tuple-element.482), channel_id=1, source_target_pairs={{0,1},{1,2},{2,3},{3,4},{4,5},{5,6},{6,7},{7,8},{8,9},{9,10},{10,1... | collective-permute-start | bytes 1769480 | tf_op jit(solution)/shard_map/while/body/eval_jaxpr/ppermute | solution.py:11
  308.0 17.6 %collective-permute-start.3 = (f32[128,1152]{1,0:T(8,128)}, f32[128,1152]{1,0:T(8,128)S(1)}, u32[]{:S(2)}, u32[]{:S(2)}) collective-permute-start(f32[128,1152]{1,0:T(8,128)} %get-tuple-element.483), channel_id=1, source_target_pairs={{0,255},{1,0},{2,1},{3,2},{4,3},{5,4},{6,5},{7,6},{8,7},{9,8},{10,... | collective-permute-start | bytes 1769480 | tf_op jit(solution)/shard_map/while/body/eval_jaxpr/ppermute | solution.py:11
  326.7 11.2 %collective-permute-start.1 = (bf16[128,1152]{1,0:T(8,128)(2,1)}, bf16[128,1152]{1,0:T(8,128)(2,1)S(1)}, u32[]{:S(2)}, u32[]{:S(2)}) collective-permute-start(bf16[128,1152]{1,0:T(8,128)(2,1)} %get-tuple-element.481), channel_id=1, source_target_pairs={{0,255},{1,0},{2,1},{3,2},{4,3},{5,4},{6,5},{7,6},{8,7},{9,8},{10,... | collective-permute-start | bytes 884744 | tf_op jit(solution)/shard_map/while/body/eval_jaxpr/ppermute | solution.py:11
  326.7 12.5 %collective-permute-start = (bf16[128,1152]{1,0:T(8,128)(2,1)}, bf16[128,1152]{1,0:T(8,128)(2,1)S(1)}, u32[]{:S(2)}, u32[]{:S(2)}) collective-permute-start(bf16[128,1152]{1,0:T(8,128)(2,1)} %get-tuple-element.480), channel_id=1, source_target_pairs={{0,1},{1,2},{2,3},{3,4},{4,5},{5,6},{6,7},{7,8},{8,9},{9,10},{10,1... | collective-permute-start | bytes 884744 | tf_op jit(solution)/shard_map/while/body/eval_jaxpr/ppermute | solution.py:11
  331.0 18.9 %collective-permute-start.2 = (f32[128,1152]{1,0:T(8,128)}, f32[128,1152]{1,0:T(8,128)}, u32[]{:S(2)}, u32[]{:S(2)}) collective-permute-start(f32[128,1152]{1,0:T(8,128)} %get-tuple-element.482), channel_id=1, source_target_pairs={{0,1},{1,2},{2,3},{3,4},{4,5},{5,6},{6,7},{7,8},{8,9},{9,10},{10,1... | collective-permute-start | bytes 1769480 | tf_op jit(solution)/shard_map/while/body/eval_jaxpr/ppermute | solution.py:11
  334.4 17.7 %collective-permute-start.3 = (f32[128,1152]{1,0:T(8,128)}, f32[128,1152]{1,0:T(8,128)S(1)}, u32[]{:S(2)}, u32[]{:S(2)}) collective-permute-start(f32[128,1152]{1,0:T(8,128)} %get-tuple-element.483), channel_id=1, source_target_pairs={{0,255},{1,0},{2,1},{3,2},{4,3},{5,4},{6,5},{7,6},{8,7},{9,8},{10,... | collective-permute-start | bytes 1769480 | tf_op jit(solution)/shard_map/while/body/eval_jaxpr/ppermute | solution.py:11
  353.2 12.4 %collective-permute-start.1 = (bf16[128,1152]{1,0:T(8,128)(2,1)}, bf16[128,1152]{1,0:T(8,128)(2,1)S(1)}, u32[]{:S(2)}, u32[]{:S(2)}) collective-permute-start(bf16[128,1152]{1,0:T(8,128)(2,1)} %get-tuple-element.481), channel_id=1, source_target_pairs={{0,255},{1,0},{2,1},{3,2},{4,3},{5,4},{6,5},{7,6},{8,7},{9,8},{10,... | collective-permute-start | bytes 884744 | tf_op jit(solution)/shard_map/while/body/eval_jaxpr/ppermute | solution.py:11
  353.2 13.6 %collective-permute-start = (bf16[128,1152]{1,0:T(8,128)(2,1)}, bf16[128,1152]{1,0:T(8,128)(2,1)S(1)}, u32[]{:S(2)}, u32[]{:S(2)}) collective-permute-start(bf16[128,1152]{1,0:T(8,128)(2,1)} %get-tuple-element.480), channel_id=1, source_target_pairs={{0,1},{1,2},{2,3},{3,4},{4,5},{5,6},{6,7},{7,8},{8,9},{9,10},{10,1... | collective-permute-start | bytes 884744 | tf_op jit(solution)/shard_map/while/body/eval_jaxpr/ppermute | solution.py:11
  358.0 19.5 %collective-permute-start.2 = (f32[128,1152]{1,0:T(8,128)}, f32[128,1152]{1,0:T(8,128)}, u32[]{:S(2)}, u32[]{:S(2)}) collective-permute-start(f32[128,1152]{1,0:T(8,128)} %get-tuple-element.482), channel_id=1, source_target_pairs={{0,1},{1,2},{2,3},{3,4},{4,5},{5,6},{6,7},{7,8},{8,9},{9,10},{10,1... | collective-permute-start | bytes 1769480 | tf_op jit(solution)/shard_map/while/body/eval_jaxpr/ppermute | solution.py:11
  361.4 18.3 %collective-permute-start.3 = (f32[128,1152]{1,0:T(8,128)}, f32[128,1152]{1,0:T(8,128)S(1)}, u32[]{:S(2)}, u32[]{:S(2)}) collective-permute-start(f32[128,1152]{1,0:T(8,128)} %get-tuple-element.483), channel_id=1, source_target_pairs={{0,255},{1,0},{2,1},{3,2},{4,3},{5,4},{6,5},{7,6},{8,7},{9,8},{10,... | collective-permute-start | bytes 1769480 | tf_op jit(solution)/shard_map/while/body/eval_jaxpr/ppermute | solution.py:11
  380.8 50.6 %copy-start.8 = (f32[128]{0:T(128)}, f32[128]{0:T(128)S(1)}, u32[]{:S(2)}) copy-start(f32[128]{0:T(128)S(1)} %get-tuple-element.319) | copy-start | bytes 1540
  380.8 17.9 %collective-permute-start.9 = (f32[128,1152]{1,0:T(8,128)}, f32[128,1152]{1,0:T(8,128)S(1)}, u32[]{:S(2)}, u32[]{:S(2)}) collective-permute-start(f32[128,1152]{1,0:T(8,128)} %get-tuple-element.322), channel_id=1, source_target_pairs={{0,255},{1,0},{2,1},{3,2},{4,3},{5,4},{6,5},{7,6},{8,7},{9,8},{10,... | collective-permute-start | bytes 1769480 | tf_op jit(solution)/shard_map/ppermute | solution.py:11
  399.9 15.2 %collective-permute-start.10 = (f32[128,1152]{1,0:T(8,128)S(1)}, f32[128,1152]{1,0:T(8,128)S(1)}, u32[]{:S(2)}, u32[]{:S(2)}) collective-permute-start(f32[128,1152]{1,0:T(8,128)S(1)} %add.355), channel_id=1, source_target_pairs={{0,249},{1,250},{2,251},{3,252},{4,253},{5,254},{6,255},{7,0},{8,1... | collective-permute-start | bytes 1769480 | tf_op jit(solution)/shard_map/ppermute | solution.py:11
  415.1 16.2 %collective-permute-start.11 = (f32[128,1152]{1,0:T(8,128)S(1)}, f32[128,1152]{1,0:T(8,128)S(1)}, u32[]{:S(2)}, u32[]{:S(2)}) collective-permute-start(f32[128,1152]{1,0:T(8,128)S(1)} %collective-permute-done.10), channel_id=1, source_target_pairs={{0,240},{1,241},{2,242},{3,243},{4,244},{5,245},{6,246},{7,247},{8... | collective-permute-start | bytes 1769480 | tf_op jit(solution)/shard_map/ppermute | solution.py:11
  431.4 16.4 %collective-permute-start.12 = (f32[128,1152]{1,0:T(8,128)S(1)}, f32[128,1152]{1,0:T(8,128)S(1)}, u32[]{:S(2)}, u32[]{:S(2)}) collective-permute-start(f32[128,1152]{1,0:T(8,128)S(1)} %broadcast_select_fusion.4), channel_id=1, source_target_pairs={{0,224},{1,225},{2,226},{3,227},{4,228},{5,229},{6,230},{7,231},{8... | collective-permute-start | bytes 1769480 | tf_op jit(solution)/shard_map/ppermute | solution.py:11
  447.9 28.8 %copy-start.2 = (f32[128,2304]{1,0:T(8,128)S(1)}, f32[128,2304]{1,0:T(8,128)}, u32[]{:S(2)}) copy-start(f32[128,2304]{1,0:T(8,128)} %reduce-scatter.2.cloned.1.call-done) | copy-start | bytes 3538948
  447.9 28.8 %copy-start.4 = (bf16[128,1152]{1,0:T(8,128)(2,1)S(1)}, bf16[128,1152]{1,0:T(8,128)(2,1)}, u32[]{:S(2)}) copy-start(bf16[128,1152]{1,0:T(8,128)(2,1)} %param.13) | copy-start | bytes 884740
  447.9 14.0 %collective-permute-start.13 = (f32[128,1152]{1,0:T(8,128)S(1)}, f32[128,1152]{1,0:T(8,128)S(1)}, u32[]{:S(2)}, u32[]{:S(2)}) collective-permute-start(f32[128,1152]{1,0:T(8,128)S(1)} %broadcast_select_fusion.5), channel_id=1, source_target_pairs={{0,192},{1,193},{2,194},{3,195},{4,196},{5,197},{6,198},{7,199},{8... | collective-permute-start | bytes 1769480 | tf_op jit(solution)/shard_map/ppermute | solution.py:11
  462.0 14.7 %collective-permute-start.14 = (f32[128,1152]{1,0:T(8,128)S(1)}, f32[128,1152]{1,0:T(8,128)S(1)}, u32[]{:S(2)}, u32[]{:S(2)}) collective-permute-start(f32[128,1152]{1,0:T(8,128)S(1)} %broadcast_select_fusion.6), channel_id=1, source_target_pairs={{0,128},{1,129},{2,130},{3,131},{4,132},{5,133},{6,134},{7,135},{8... | collective-permute-start | bytes 1769480 | tf_op jit(solution)/shard_map/ppermute | solution.py:11
  (1 other events, 1.3 us)
Sparse Core Ops, SparseCore 0:
  21.9 103.6 reduce-scatter.1
where the time goes:
time: 493 us; the launch traced here: 485 us
  waiting for transfers between devices  334 us (68%)
  starting transfers between devices  59.5 us (12%)
  matrix products  51 us (10%)
  between operations  16.3 us (3%)
  local copies, waits for them, and re-layouts  12.2 us (2%)
  other arithmetic  12 us (2%)
    ppermute x39, waiting for transfers between devices, shifted(): lax.ppermute(shard, axis, [(i, (i + by) % devices) for i in range(devices)])  230 us
    reduce_scatter x1, waiting for transfers between devices, body(): lax.psum_scatter(jnp.concatenate([jnp.dot(img_hidden, img_down, preferred...  104 us
    ppermute x39, starting transfers between devices, shifted(): lax.ppermute(shard, axis, [(i, (i + by) % devices) for i in range(devices)])  59.5 us
    dot_general x16, matrix products, pair_tile(): lax.dot_general(coef, image_low, (((0,), (0,)), ((), ())), preferred_elem...  25 us
    dot_general x16, matrix products, pair_tile(): lax.dot_general(image_low, text_block, (((1,), (1,)), ((), ())), preferre...  13.8 us
    while x14, local copies, waits for them, and re-layouts  10 us
  transfers between devices with their start and end apart: 40, of which 30 were waited for; matrix products, arithmetic and copies ran while one was open for 9% of the time, Pallas kernels for 0%

commit v1 on v0

v1 whole, which is shorter than its diff:
```python
import jax
import jax.numpy as jnp
from jax import lax
from jax.sharding import Mesh, PartitionSpec as P

STEPS = 16
ROWS_OF = ("chip", "core")
ALL = ("chip", "core", "z")


def shifted(shard, axis, by):
    devices = lax.axis_size(axis)
    return lax.ppermute(shard, axis, [(i, (i + by) % devices) for i in range(devices)])


def shifted_by_window(shard, window, sign):
    chips = lax.axis_size("chip")

    def branch(by):
        if by == 0:
            return lambda value: value
        return lambda value: shifted(value, "chip", sign * by)

    return lax.switch(window, [branch(by) for by in range(chips)], shard)


def unit_rows(emb):
    length = jnp.sqrt(jnp.sum(emb * emb, axis=1, keepdims=True) + 1e-06)
    return (emb / length, length)


def logits(rows, columns, scale, shift_value):
    cosine = lax.dot_general(
        rows, columns, (((1,), (1,)), ((), ())), preferred_element_type=jnp.float32
    )
    return scale * cosine + shift_value


def coefs(logit, positive, scale):
    return ((jax.nn.sigmoid(logit) - positive.astype(jnp.float32)) * scale).astype(jnp.bfloat16)


def body(
    img_hidden, img_down, img_pooled, txt_hidden, txt_proj, log_temp, bias, match, window_index
):
    rows = img_pooled.shape[0]
    scale = jnp.exp(log_temp[0])
    shift_value = bias[0]
    window = window_index[0]
    place = lax.axis_index(ALL)
    devices = lax.axis_size(ALL)
    z = lax.axis_index("z")
    z_size = lax.axis_size("z")
    core = lax.axis_index("core")

    half = txt_proj.shape[0] // 2
    proj_half = lax.dynamic_slice_in_dim(txt_proj, core * half, half, 0)
    proj = lax.all_gather(proj_half, ("z", "core"), axis=0, tiled=True)

    img_part = jnp.dot(img_hidden, img_down, preferred_element_type=jnp.float32)
    img_sum = lax.psum_scatter(img_part, "z", scatter_dimension=0, tiled=True)

    hidden = shifted_by_window(txt_hidden.T, window, 1)
    hidden = lax.all_gather(hidden, "z", axis=0, tiled=True)
    txt_emb = lax.dot_general(
        hidden, proj, (((0,), (0,)), ((), ())), preferred_element_type=jnp.float32
    )
    txt_unit_all, txt_len_all = unit_rows(txt_emb)
    text_0 = txt_unit_all.astype(jnp.bfloat16)
    text_1 = shifted(text_0, ROWS_OF, 1)
    text_2 = shifted(text_1, ROWS_OF, 1)

    matches = match
    for level in range(4):
        matches = jnp.concatenate([matches, shifted(matches, ALL, -(1 << level))])

    img_emb = img_sum + img_pooled.astype(jnp.float32)
    img_unit, img_len = unit_rows(img_emb)
    image_low = img_unit.astype(jnp.bfloat16)
    image_0 = lax.all_gather(image_low, "z", axis=0, tiled=True)
    image_2 = lax.all_gather(shifted(image_low, ROWS_OF, -2), "z", axis=0, tiled=True)
    image_1 = shifted(image_0, ROWS_OF, -1)

    row_iota = lax.iota(jnp.int32, z_size * rows)
    block_of = row_iota // rows
    column_base = (place - z) * rows
    total_rows = devices * rows
    window_rows = window * STEPS * rows

    text_near = jnp.where((block_of <= z)[:, None], text_0, text_2)
    near_index = column_base + row_iota - jnp.where(block_of <= z, 0, 2 * z_size * rows)
    near_index = (near_index - window_rows) % total_rows
    far_index = (column_base + row_iota - z_size * rows - window_rows) % total_rows

    def image_side(columns, index):
        positive = match[:, None] == index[None, :]
        logit = logits(image_low, columns, scale, shift_value)
        loss = jnp.sum(
            jnp.where(positive, jax.nn.softplus(-logit), jax.nn.softplus(logit)), axis=1
        )
        coef = coefs(logit, positive, scale)
        return loss, jnp.dot(coef, columns, preferred_element_type=jnp.float32)

    loss_near, part_near = image_side(text_near, near_index)
    loss_far, part_far = image_side(text_1, far_index)
    row_loss = loss_near + loss_far
    image_dunit = part_near + part_far
    img_grad = (
        image_dunit - img_unit * jnp.sum(img_unit * image_dunit, axis=1, keepdims=True)
    ) / img_len

    txt_unit = lax.dynamic_slice_in_dim(txt_unit_all, z * rows, rows, 0)
    txt_len = lax.dynamic_slice_in_dim(txt_len_all, z * rows, rows, 0)
    text_low = txt_unit.astype(jnp.bfloat16)
    own_index = (place * rows - window_rows) % total_rows + lax.iota(jnp.int32, rows)

    image_near = jnp.where((block_of >= z)[:, None], image_0, image_2)
    near_match = lax.dynamic_slice_in_dim(
        jnp.concatenate([matches, matches]), (2 * z_size - z) * rows, z_size * rows
    )
    far_match = lax.dynamic_slice_in_dim(matches, (z_size - z) * rows, z_size * rows)

    def text_side(columns, index):
        positive = own_index[:, None] == index[None, :]
        coef = coefs(logits(text_low, columns, scale, shift_value), positive, scale)
        return jnp.dot(coef, columns, preferred_element_type=jnp.float32)

    text_dunit = text_side(image_near, near_match) + text_side(image_1, far_match)
    txt_grad = (
        text_dunit - txt_unit * jnp.sum(txt_unit * text_dunit, axis=1, keepdims=True)
    ) / txt_len
    txt_grad = shifted_by_window(txt_grad, window, -1)
    return (img_grad, txt_grad, row_loss)


def solution(mesh):
    z_size = mesh.shape["tensor"]
    fine = Mesh(mesh.devices.reshape(-1, 2, z_size), ALL)
    in_specs = (
        P(ROWS_OF, "z"),
        P("z", None),
        P(ALL, None),
        P(ROWS_OF, "z"),
        P("z", None),
        P(),
        P(),
        P(ALL),
        P(),
    )
    out_specs = (P(ALL, None), P(ALL, None), P(ALL))
    return jax.shard_map(body, mesh=fine, in_specs=in_specs, out_specs=out_specs, check_vma=False)
```

time: 493 us -> 325 us (0.66)
  waiting for transfers between devices: 334 us -> 206 us
  matrix products: 51 us -> 34.7 us
  starting transfers between devices: 59.5 us -> 47.3 us
  local copies, waits for them, and re-layouts: 12.2 us -> 5.82 us
    ppermute x39 -> x10, waiting for transfers between devices: 230 us -> 75.6 us  [shifted(): lax.ppermute(shard, axis, [(i, (i + by) % devices) for i in range(devices)])]
    all_gather x0 -> x4, waiting for transfers between devices: none -> 76.3 us  [the longest x1 40.7 us: body(): proj = lax.all_gather(proj_half, ('z', 'core'), axis=0, tiled=True)]
    reduce_scatter x1, waiting for transfers between devices: 104 us -> 53.6 us  [body(): img_sum = lax.psum_scatter(img_part, 'z', scatter_dimension=0, tiled=True)]
    dot_general x50 -> x8, matrix products: 51 us -> 34.7 us  [the longest x2 9.76 us: text_side(): return jnp.dot(coef, columns, preferred_element_type=jnp.float32)]
    ppermute x39 -> x10, starting transfers between devices: 59.5 us -> 46.9 us  [shifted(): lax.ppermute(shard, axis, [(i, (i + by) % devices) for i in range(devices)])]
    while x14 -> x0, local copies, waits for them, and re-layouts: 10 us -> none
    concatenate x1 -> x3, other arithmetic: 6.7 us -> 0.02 us  [body(): matches = jnp.concatenate([matches, shifted(matches, ALL, -(1 << level))])]
    convert_element_type x0 -> x1, other arithmetic: none -> 5.2 us  [body(): text_0 = txt_unit_all.astype(jnp.bfloat16)]
  transfers between devices with their start and end apart: 40 -> 15, of which waited for: 30 -> 11; matrix products, arithmetic and copies ran while one was open for 9% -> 11% of each run, Pallas kernels for 0% -> 0%
where the time goes in v1:
time: 325 us; the launch traced here: 321 us
  waiting for transfers between devices  206 us (63%)
  starting transfers between devices  47.3 us (15%)
  matrix products  34.7 us (11%)
  between operations  16.3 us (5%)
  other arithmetic  11.2 us (3%)
  local copies, waits for them, and re-layouts  5.82 us (2%)
    ppermute x10, waiting for transfers between devices, shifted(): lax.ppermute(shard, axis, [(i, (i + by) % devices) for i in range(devices)])  75.6 us
    reduce_scatter x1, waiting for transfers between devices, body(): img_sum = lax.psum_scatter(img_part, 'z', scatter_dimension=0, tiled=True)  53.6 us
    ppermute x10, starting transfers between devices, shifted(): lax.ppermute(shard, axis, [(i, (i + by) % devices) for i in range(devices)])  46.9 us
    all_gather x1, waiting for transfers between devices, body(): proj = lax.all_gather(proj_half, ('z', 'core'), axis=0, tiled=True)  40.7 us
    all_gather x1, waiting for transfers between devices, body(): hidden = lax.all_gather(hidden, 'z', axis=0, tiled=True)  35.6 us
    dot_general x2, matrix products, text_side(): return jnp.dot(coef, columns, preferred_element_type=jnp.float32)  9.76 us
    dot_general x1, matrix products, body(): lax.dot_general(hidden, proj, (((0,), (0,)), ((), ())), preferred_element...  8.2 us
    dot_general x2, matrix products, logits(): lax.dot_general(rows, columns, (((1,), (1,)), ((), ())), preferred_elemen...  7.14 us
  transfers between devices with their start and end apart: 15, of which 11 were waited for; matrix products, arithmetic and copies ran while one was open for 11% of the time, Pallas kernels for 0%

profile of v1, /device:TPU:192, one launch (start us, length us, event | category | flops | bytes accessed | tf_op | source)
XLA Modules:
  0.0 321.2 jit_solution(5283893494571693652)
XLA Ops:
  7.2 1.1 copy.63
  9.0 12.1 %conditional.2 = (bf16[144,1024]{1,0:T(8,128)(2,1)S(1)}) conditional(s32[]{:T(128)} %bitcast.1, bf16[144,1024]{1,0:T(8,128)(2,1)S(1)} %bitcast.19, bf16[144,1024]{1,0:T(8,128)(2,1)S(1)} %bitcast.20, bf16[144,1024]{1,0:T(8,128)(2,1)S(1)} %bitcast.21, bf16[144,1024]{1,0:T(8,128)(2,1)S(1)} %bitcast.22, ...), branch_computations={%region_2.0_spmd, %region_3.0_spmd, %region_4.0_spmd, %region_5.0_... | conditional | bytes 1769520 | solution.py:24
  9.0 5.7 %collective-permute-start.9 = (bf16[144,1024]{1,0:T(8,128)(2,1)S(1)}, bf16[144,1024]{1,0:T(8,128)(2,1)S(1)}, u32[]{:S(2)}, u32[]{:S(2)}) collective-permute-start(bf16[144,1024]{1,0:T(8,128)(2,1)S(1)} %param.10), channel_id=1, source_target_pairs={{0,160},{16,176},{32,192},{48,208},{64,224},{80,240},{96,0},{112,1... | collective-permute-start | bytes 884744 | tf_op jit(solution)/shard_map/cond/branch_10_fun/ppermute | solution.py:13
  14.7 6.3 %collective-permute-done.9 = bf16[144,1024]{1,0:T(8,128)(2,1)S(1)} collective-permute-done((bf16[144,1024]{1,0:T(8,128)(2,1)S(1)}, bf16[144,1024]{1,0:T(8,128)(2,1)S(1)}, u32[]{:S(2)}, u32[]{:S(2)}) %collective-permute-start.9) | collective-permute-done | bytes 294944 | tf_op jit(solution)/shard_map/cond/branch_10_fun/ppermute | solution.py:13
  21.1 0.7 copy-done.5
  21.8 0.0 all-gather.7.cloned.1.call-start
  21.8 0.7 constant_dynamic-slice_fusion
  22.6 0.3 reduce-scatter.2.cloned.1.call-start
  22.9 4.4 %fusion.74 = f32[1024,1152]{1,0:T(8,128)} fusion(bf16[1024,538]{0,1:T(8,128)(2,1)S(1)} %copy-done.11, bf16[538,1152]{1,0:T(8,128)(2,1)S(1)} %copy-done), kind=kOutput, calls=%fused_computation.132 | convolution fusion | flops 1269301248 | bytes 7059968 | tf_op jit(solution)/shard_map/dot_general | solution.py:60
  27.3 0.0 all-gather.9.cloned.1.call-start
  27.4 35.6 %all-gather.5.cloned.1.call-done = bf16[1152,1024]{1,0:T(8,128)(2,1)} async-done(((bf16[144,1024]{1,0:T(8,128)(2,1)}), bf16[1152,1024]{1,0:T(8,128)(2,1)}) %all-gather.5.cloned.1.call-update) | async-done | bytes 2359312 | tf_op jit(solution)/shard_map/all_gather | solution.py:64
  63.0 40.7 %all-gather.7.cloned.1.call-done = bf16[1152,1152]{1,0:T(8,128)(2,1)} async-done(((bf16[72,1152]{1,0:T(8,128)(2,1)}), bf16[1152,1152]{1,0:T(8,128)(2,1)}) %all-gather.7.cloned.1.call-update) | async-done | bytes 2654224 | tf_op jit(solution)/shard_map/all_gather | solution.py:58
  103.7 8.2 %multiply_reduce_fusion = (f32[1024]{0:T(1024)S(1)}, f32[1024,1152]{1,0:T(8,128)}) fusion(bf16[1152,1024]{1,0:T(8,128)(2,1)} %all-gather.5.cloned.1.call-done, bf16[1152,1152]{1,0:T(8,128)(2,1)} %all-gather.7.cloned.1.call-done), kind=kOutput, calls=%fused_computation | convolution fusion | flops 2720267264 | bytes 9736192 | tf_op jit(solution)/shard_map/dot_general | solution.py:65
  111.9 53.6 %reduce-scatter.2.cloned.1.call-done = f32[128,1152]{1,0:T(8,128)} async-done(((f32[1024,1152]{1,0:T(8,128)}), f32[128,1152]{1,0:T(8,128)}) %reduce-scatter.2.cloned.1.call-update) | async-done | bytes 589840 | tf_op jit(solution)/shard_map/reduce_scatter | solution.py:61
  165.5 1.2 multiply_reduce_fusion.3
  166.7 1.9 fusion.72
  168.7 0.0 all-gather.11.cloned.1.call-start
  168.7 5.2 %fusion.73 = (bf16[1024,1152]{1,0:T(8,128)(2,1)S(1)}, f32[1024,1152]{1,0:T(8,128)}) fusion(f32[1024,1152]{1,0:T(8,128)} %get-tuple-element.84, f32[1024]{0:T(1024)S(1)} %add_sqrt_fusion), kind=kLoop, calls=%fused_computation.131 | loop fusion | flops 2359296 | bytes 11800576 | tf_op jit(solution)/shard_map/convert_element_type | solution.py:69
  173.9 1.5 copy-done.3
  175.4 31.7 %collective-permute-done.30 = bf16[1024,1152]{1,0:T(8,128)(2,1)} collective-permute-done((bf16[1024,1152]{1,0:T(8,128)(2,1)S(1)}, bf16[1024,1152]{1,0:T(8,128)(2,1)}, u32[]{:S(2)}, u32[]{:S(2)}) %collective-permute-start.30) | collective-permute-done | bytes 2359328 | tf_op jit(solution)/shard_map/ppermute | solution.py:13
  207.1 1.4 collective-permute-start.33
  209.8 1.6 collective-permute-start.32
  211.5 5.3 %collective-permute-done.32 = bf16[128,1152]{1,0:T(8,128)(2,1)S(1)} collective-permute-done((bf16[128,1152]{1,0:T(8,128)(2,1)S(1)}, bf16[128,1152]{1,0:T(8,128)(2,1)S(1)}, u32[]{:S(2)}, u32[]{:S(2)}) %collective-permute-start.32) | collective-permute-done | bytes 294944 | tf_op jit(solution)/shard_map/ppermute | solution.py:13
  216.8 0.7 copy-done.8
  217.6 2.8 collective-permute-start.34
  220.4 2.5 collective-permute-done.34
  222.9 4.7 %collective-permute-start.35 = (s32[512]{0:T(512)S(1)}, s32[512]{0:T(512)S(1)}, u32[]{:S(2)}, u32[]{:S(2)}) collective-permute-start(s32[512]{0:T(512)S(1)} %pad_add_fusion.1), channel_id=1, source_target_pairs={{0,252},{1,253},{2,254},{3,255},{4,0},{5,1},{6,2},{7,3},{8,4},{9,5... | collective-permute-start | bytes 6152 | tf_op jit(solution)/shard_map/ppermute | solution.py:13
  227.6 2.2 collective-permute-done.35
  229.8 25.4 %collective-permute-start.36 = (s32[1024]{0:T(1024)S(1)}, s32[1024]{0:T(1024)S(1)}, u32[]{:S(2)}, u32[]{:S(2)}) collective-permute-start(s32[1024]{0:T(1024)S(1)} %pad_add_fusion), channel_id=1, source_target_pairs={{0,248},{1,249},{2,250},{3,251},{4,252},{5,253},{6,254},{7,255},{8... | collective-permute-start | bytes 12296 | tf_op jit(solution)/shard_map/ppermute | solution.py:13
  255.3 1.3 collective-permute-done.36
  256.7 5.1 %collective-permute-start.37 = (bf16[1024,1152]{1,0:T(8,128)(2,1)}, bf16[1024,1152]{1,0:T(8,128)(2,1)}, u32[]{:S(2)}, u32[]{:S(2)}) collective-permute-start(bf16[1024,1152]{1,0:T(8,128)(2,1)} %all-gather.9.cloned.1.call-done), channel_id=1, source_target_pairs={{0,248},{8,0},{16,8},{24,16},{32,24},{40,32},{48,40},{56,48},{64,5... | collective-permute-start | bytes 7077896 | tf_op jit(solution)/shard_map/ppermute | solution.py:13
  261.8 0.1 dynamic_slice.16
  261.8 0.1 dynamic_slice.15
  261.9 0.1 dynamic-slice.3
  262.0 3.4 %fusion.15 = f32[128,1024]{1,0:T(8,128)S(1)} fusion(bf16[128,1152]{1,0:T(8,128)(2,1)S(1)} %copy-done.6, f32[]{:T(128)} %bitcast.15, f32[]{:T(128)} %bitcast, bf16[1024,1152]{1,0:T(8,128)(2,1)} %copy-done.3, bf16[1024,1152]{1,0:T(8,128)(2,1)} %collective-permute-done.31, pred[1024]{0:T(1024)(128)(4,1)S(1)} %fusion.62), kind=kOutput, calls=%fused_computation.29 | convolution fusion | flops 303431680 | bytes 5538824 | tf_op jit(solution)/shard_map/dot_general | solution.py:33
  265.4 3.8 %fusion.26 = (f32[128]{0:T(128)S(1)}, f32[128]{0:T(128)S(1)}, f32[128,1024]{1,0:T(8,128)S(1)}) fusion(s32[1024]{0:T(1024)S(1)} %get-tuple-element.90, s32[128]{0:T(128)S(1)} %copy-done.10, f32[128,1024]{1,0:T(8,128)S(1)} %fusion.15, s32[1024]{0:T(1024)S(1)} %get-tuple-element.91, f32[]{:T(128)} %bitcast.18, bf16[128,1152]{1,0:T(8,128)(2,1)S(1)} %copy-done.6, ...), kind=kOutput, calls=%fused_computation.50 | convolution fusion | flops 306446080 | bytes 3712520 | tf_op jit(solution)/shard_map/dot_general | solution.py:33
  269.2 0.5 add.200
  269.7 2.5 fusion.36
  272.2 2.7 multiply_reduce_fusion.2
  274.9 1.0 subtract_divide_fusion.1
  276.0 12.5 %collective-permute-done.37 = bf16[1024,1152]{1,0:T(8,128)(2,1)} collective-permute-done((bf16[1024,1152]{1,0:T(8,128)(2,1)}, bf16[1024,1152]{1,0:T(8,128)(2,1)}, u32[]{:S(2)}, u32[]{:S(2)}) %collective-permute-start.37) | collective-permute-done | bytes 2359328 | tf_op jit(solution)/shard_map/ppermute | solution.py:13
  288.4 3.9 %fusion.18 = f32[128,1152]{1,0:T(8,128)S(1)} fusion(bf16[1024,1152]{1,0:T(8,128)(2,1)} %collective-permute-done.37, s32[1024]{0:T(1024)S(1)} %dynamic_slice.16, f32[]{:T(128)} %bitcast.16, f32[]{:T(128)} %bitcast, s32[128]{0:T(128)S(1)} %iota_add_fusion.1, f32[1024,1152]{1,0:T(8,128)} %get-tuple-element.72, s32[]{:T(128)S(6)} %select_n.97), kind=kOutput, calls=%fused_computation.32 | convolution fusion | flops 605290496 | bytes 5608964 | tf_op jit(solution)/shard_map/dot_general | solution.py:126
  292.4 5.9 %multiply_reduce_fusion.1 = (f32[128]{0:T(128)S(1)}, f32[128,1152]{1,0:T(8,128)S(1)}) fusion(f32[1024,1152]{1,0:T(8,128)} %get-tuple-element.72, s32[]{:T(128)S(6)} %select_n.97, f32[128,1152]{1,0:T(8,128)S(1)} %fusion.18, bf16[1024,1152]{1,0:T(8,128)(2,1)} %all-gather.9.cloned.1.call-done, bf16[1024,1152]{1,0:T(8,128)(2,1)} %all-gather.11.cloned.1.call-done, ...), kind=kOutput, calls=%fused_computation.38 | convolution fusion | flops 608092032 | bytes 11510784 | tf_op jit(solution)/shard_map/dot_general | solution.py:126
  298.2 1.2 subtract_divide_fusion
  299.5 14.2 %conditional.3 = (f32[128,1152]{1,0:T(8,128)S(1)}) conditional(s32[]{:T(128)} %bitcast.1, f32[128,1152]{1,0:T(8,128)S(1)} %subtract_divide_fusion, f32[128,1152]{1,0:T(8,128)S(1)} %subtract_divide_fusion, f32[128,1152]{1,0:T(8,128)S(1)} %subtract_divide_fusion, f32[128,1152]{1,0:T(8,128)S(1)} %subtract_divide_fusion, ...), branch_computations={%region_21.22_spmd, %region_22.23_spmd, %region_23.24_spmd, %regio... | conditional | bytes 3538992 | solution.py:24
  299.7 0.1 collective-permute-start.24
  299.8 13.8 %collective-permute-done.24 = f32[128,1152]{1,0:T(8,128)S(1)} collective-permute-done((f32[128,1152]{1,0:T(8,128)S(1)}, f32[128,1152]{1,0:T(8,128)S(1)}, u32[]{:S(2)}, u32[]{:S(2)}) %collective-permute-start.24) | collective-permute-done | bytes 589856 | tf_op jit(solution)/shard_map/cond/branch_10_fun/ppermute | solution.py:13
  313.7 0.8 copy-done.7
  (55 shorter events, 0.4 us)
Async XLA Ops:
  7.2 15.7 %copy-start = (bf16[538,1152]{1,0:T(8,128)(2,1)S(1)}, bf16[538,1152]{1,0:T(8,128)(2,1)}, u32[]{:S(2)}) copy-start(bf16[538,1152]{1,0:T(8,128)(2,1)} %param.42) | copy-start | bytes 3718660
  7.2 55.8 %all-gather.5.cloned.1.call-start = ((), (), s32[]{:S(2)}) async-start(), calls=%async_computation.2 | async-start | bytes 2654208 | tf_op jit(solution)/shard_map/all_gather | solution.py:64
  8.9 12.9 %copy-start.9 = (bf16[144,1152]{1,0:T(8,128)(2,1)S(1)}, bf16[144,1152]{1,0:T(8,128)(2,1)}, u32[]{:S(2)}) copy-start(bf16[144,1152]{1,0:T(8,128)(2,1)} %param.45) | copy-start | bytes 995332
  8.9 13.9 %copy-start.11 = (bf16[1024,538]{0,1:T(8,128)(2,1)S(1)}, bf16[1024,538]{0,1:T(8,128)(2,1)}, u32[]{:S(2)}) copy-start(bf16[1024,538]{0,1:T(8,128)(2,1)} %param.41) | copy-start | bytes 3305476
  9.0 12.0 %collective-permute-start.9 = (bf16[144,1024]{1,0:T(8,128)(2,1)S(1)}, bf16[144,1024]{1,0:T(8,128)(2,1)S(1)}, u32[]{:S(2)}, u32[]{:S(2)}) collective-permute-start(bf16[144,1024]{1,0:T(8,128)(2,1)S(1)} %param.10), channel_id=1, source_target_pairs={{0,160},{16,176},{32,192},{48,208},{64,224},{80,240},{96,0},{112,1... | collective-permute-start | bytes 884744 | tf_op jit(solution)/shard_map/cond/branch_10_fun/ppermute | solution.py:13
  21.0 0.7 copy-start.5
  21.8 81.9 %all-gather.7.cloned.1.call-start = ((), (), s32[]{:S(2)}) async-start(), calls=%async_computation.3 | async-start | bytes 2820096 | tf_op jit(solution)/shard_map/all_gather | solution.py:58
  22.6 142.9 %reduce-scatter.2.cloned.1.call-start = ((), (), s32[]{:S(2)}) async-start(), calls=%async_computation.1 | async-start | bytes 5308416 | tf_op jit(solution)/shard_map/reduce_scatter | solution.py:61
  27.3 138.2 %copy-start.2 = (bf16[128,1152]{1,0:T(8,128)(2,1)S(1)}, bf16[128,1152]{1,0:T(8,128)(2,1)}, u32[]{:S(2)}) copy-start(bf16[128,1152]{1,0:T(8,128)(2,1)} %param.43) | copy-start | bytes 884740
  27.3 229.3 %all-gather.9.cloned.1.call-start = ((), (), s32[]{:S(2)}) async-start(), calls=%async_computation.4 | async-start | bytes 2654208 | tf_op jit(solution)/shard_map/all_gather | solution.py:80
  168.7 123.7 %all-gather.11.cloned.1.call-start = ((), (), s32[]{:S(2)}) async-start(), calls=%async_computation.5 | async-start | bytes 2654208 | tf_op jit(solution)/shard_map/all_gather | solution.py:81
  168.7 38.4 %copy-start.10 = (s32[128]{0:T(128)S(1)}, s32[128]{0:T(128)}, u32[]{:S(2)}) copy-start(s32[128]{0:T(128)} %param.48) | copy-start | bytes 1540
  168.7 41.1 %copy-start.6 = (bf16[128,1152]{1,0:T(8,128)(2,1)S(1)}, bf16[128,1152]{1,0:T(8,128)(2,1)}, u32[]{:S(2)}) copy-start(bf16[128,1152]{1,0:T(8,128)(2,1)} %fusion.72) | copy-start | bytes 884740
  173.9 1.5 copy-start.3
  175.4 31.7 %collective-permute-start.30 = (bf16[1024,1152]{1,0:T(8,128)(2,1)S(1)}, bf16[1024,1152]{1,0:T(8,128)(2,1)}, u32[]{:S(2)}, u32[]{:S(2)}) collective-permute-start(bf16[1024,1152]{1,0:T(8,128)(2,1)S(1)} %get-tuple-element.71), channel_id=1, source_target_pairs={{0,8},{8,16},{16,24},{24,32},{32,40},{40,48},{48,56},{56,64},{64,7... | collective-permute-start | bytes 7077896 | tf_op jit(solution)/shard_map/ppermute | solution.py:13
  207.1 54.9 %collective-permute-start.31 = (bf16[1024,1152]{1,0:T(8,128)(2,1)}, bf16[1024,1152]{1,0:T(8,128)(2,1)}, u32[]{:S(2)}, u32[]{:S(2)}) collective-permute-start(bf16[1024,1152]{1,0:T(8,128)(2,1)} %collective-permute-done.30), channel_id=1, source_target_pairs={{0,8},{8,16},{16,24},{24,32},{32,40},{40,48},{48,56},{56,64},{64,7... | collective-permute-start | bytes 7077896 | tf_op jit(solution)/shard_map/ppermute | solution.py:13
  207.1 10.5 %collective-permute-start.33 = (s32[128]{0:T(128)S(1)}, s32[128]{0:T(128)S(1)}, u32[]{:S(2)}, u32[]{:S(2)}) collective-permute-start(s32[128]{0:T(128)S(1)} %copy-done.10), channel_id=1, source_target_pairs={{0,255},{1,0},{2,1},{3,2},{4,3},{5,4},{6,5},{7,6},{8,7},{9,8},{10,... | collective-permute-start | bytes 1544 | tf_op jit(solution)/shard_map/ppermute | solution.py:13
  209.8 7.0 %collective-permute-start.32 = (bf16[128,1152]{1,0:T(8,128)(2,1)S(1)}, bf16[128,1152]{1,0:T(8,128)(2,1)S(1)}, u32[]{:S(2)}, u32[]{:S(2)}) collective-permute-start(bf16[128,1152]{1,0:T(8,128)(2,1)S(1)} %copy-done.6), channel_id=1, source_target_pairs={{0,240},{8,248},{16,0},{24,8},{32,16},{40,24},{48,32},{56,40},{64,... | collective-permute-start | bytes 884744 | tf_op jit(solution)/shard_map/ppermute | solution.py:13
  216.8 0.7 copy-start.8
  217.6 5.3 %collective-permute-start.34 = (s32[256]{0:T(256)S(1)}, s32[256]{0:T(256)S(1)}, u32[]{:S(2)}, u32[]{:S(2)}) collective-permute-start(s32[256]{0:T(256)S(1)} %pad_add_fusion.2), channel_id=1, source_target_pairs={{0,254},{1,255},{2,0},{3,1},{4,2},{5,3},{6,4},{7,5},{8,6},{9,7},{1... | collective-permute-start | bytes 3080 | tf_op jit(solution)/shard_map/ppermute | solution.py:13
  222.9 6.9 %collective-permute-start.35 = (s32[512]{0:T(512)S(1)}, s32[512]{0:T(512)S(1)}, u32[]{:S(2)}, u32[]{:S(2)}) collective-permute-start(s32[512]{0:T(512)S(1)} %pad_add_fusion.1), channel_id=1, source_target_pairs={{0,252},{1,253},{2,254},{3,255},{4,0},{5,1},{6,2},{7,3},{8,4},{9,5... | collective-permute-start | bytes 6152 | tf_op jit(solution)/shard_map/ppermute | solution.py:13
  229.8 26.8 %collective-permute-start.36 = (s32[1024]{0:T(1024)S(1)}, s32[1024]{0:T(1024)S(1)}, u32[]{:S(2)}, u32[]{:S(2)}) collective-permute-start(s32[1024]{0:T(1024)S(1)} %pad_add_fusion), channel_id=1, source_target_pairs={{0,248},{1,249},{2,250},{3,251},{4,252},{5,253},{6,254},{7,255},{8... | collective-permute-start | bytes 12296 | tf_op jit(solution)/shard_map/ppermute | solution.py:13
  256.7 31.8 %collective-permute-start.37 = (bf16[1024,1152]{1,0:T(8,128)(2,1)}, bf16[1024,1152]{1,0:T(8,128)(2,1)}, u32[]{:S(2)}, u32[]{:S(2)}) collective-permute-start(bf16[1024,1152]{1,0:T(8,128)(2,1)} %all-gather.9.cloned.1.call-done), channel_id=1, source_target_pairs={{0,248},{8,0},{16,8},{24,16},{32,24},{40,32},{48,40},{56,48},{64,5... | collective-permute-start | bytes 7077896 | tf_op jit(solution)/shard_map/ppermute | solution.py:13
  269.2 3.1 copy-start.1
  269.2 3.1 copy-start.4
  299.7 13.9 %collective-permute-start.24 = (f32[128,1152]{1,0:T(8,128)S(1)}, f32[128,1152]{1,0:T(8,128)S(1)}, u32[]{:S(2)}, u32[]{:S(2)}) collective-permute-start(f32[128,1152]{1,0:T(8,128)S(1)} %param.26), channel_id=1, source_target_pairs={{0,96},{16,112},{32,128},{48,144},{64,160},{80,176},{96,192},{112,... | collective-permute-start | bytes 1769480 | tf_op jit(solution)/shard_map/cond/branch_10_fun/ppermute | solution.py:13
  313.7 0.8 copy-start.7
Sparse Core Ops, SparseCore 0:
  21.9 41.0 all-gather.4
  65.4 38.2 all-gather.6
  106.2 59.2 reduce-scatter.1
  168.8 39.8 all-gather.8
  217.7 42.9 all-gather.10
